TPU v7x, 8 devices: a whole 2x2x1 slice. The times are simulated.
8 devices in a mesh: dp: 1 (over z), ep: 8 (over x, y, core).
Axes of the slice: x: 2, y: 2, z: 1, core: 2. Of those that a mesh axis runs over, the one named last changes fastest.
Arguments:
- x: bfloat16 [1, 8, 384, 2048], P('dp', 'ep')
- expert: int32 [1, 8, 384, 6], P('dp', 'ep')
- slot: int32 [1, 8, 384, 6], P('dp', 'ep')
- gate: float32 [1, 8, 384, 6], P('dp', 'ep')
- w_gate: bfloat16 [64, 2048, 1408], P('ep')
- w_up: bfloat16 [64, 2048, 1408], P('ep')
- w_down: bfloat16 [64, 1408, 2048], P('ep')
- s_gate: bfloat16 [2048, 2816], replicated
- s_up: bfloat16 [2048, 2816], replicated
- s_down: bfloat16 [2816, 2048], replicated
Outputs:
- y: bfloat16 [1, 8, 384, 2048], P('dp', 'ep')
All inputs are finite; a program needn't handle non-finite values.
Results may differ from a plain program's by a relative error of at most 0.009.
Values are sent between devices in bfloat16 or wider.
A program may use at most 2 GiB of HBM per device.

v0:
```python
import functools

import jax
import jax.numpy as jnp
from jax import lax
from jax.experimental import pallas as pl
from jax.experimental.pallas import tpu as pltpu
from jax.sharding import PartitionSpec as P

MESH = pl.DeviceIdType.MESH
F32, BF16 = jnp.float32, jnp.bfloat16
VMEM_BYTES = 67043328
PAD = 48
OWN, NEAR, FAR, RELAY, LAST, PARTNER = (0, 1, 2), (0, 1), (3, 4), (3, 4, 5, 6), (7,), (2, 5, 6, 7)


def neighbours():
    me = lax.axis_index("ep")
    core, y, x = lax.rem(me, 2), lax.rem(me // 2, 2), me // 4
    return me, me + 4 - 8 * x, me + 2 - 4 * y, me + 1 - 2 * core


def greet(devices):
    barrier = pltpu.get_barrier_semaphore()
    for device in devices:
        pl.semaphore_signal(barrier, inc=1, device_id={"ep": device}, device_id_type=MESH)
    pl.semaphore_wait(barrier, len(devices))


def dot(a, b):
    return jnp.dot(a, b, preferred_element_type=F32)


def spread(width):
    return [(n, min(n + 256, width)) for n in range(0, width, 256)]


def first_kernel(
    dims, x_hbm, meta_hbm, wg, wu, sg, su, h_out, hs_out, ct_out,
    xg, meta, acc, wbuf, z, pm, stage, ctst, xsem, wsem, osem, csem, send, recv,
):
    pieces, width, tokens, ff, own, ring = dims
    me, xn, yn, pn = neighbours()
    half = tokens // 2
    shared_steps = 2 * pieces
    total = shared_steps + pieces * own

    def copies(ref, piece, rows, kinds):
        mid = rows // 2
        low, high = pl.ds(0, mid), pl.ds(mid, mid)
        plan = (
            (ref(0), ref(1), xn), (ref(0), ref(2), yn), (ref(0), ref(4), pn),
            (ref(1).at[low], ref(3).at[low], yn), (ref(2).at[high], ref(3).at[high], xn),
            (ref(1), ref(5), pn), (ref(2), ref(6), pn), (ref(3), ref(7), pn),
        )
        return [
            pltpu.make_async_remote_copy(
                src_ref=src, dst_ref=dst, send_sem=send.at[piece, kind], recv_sem=recv.at[piece, kind],
                device_id={"ep": device}, device_id_type=MESH,
            )
            for kind, (src, dst, device) in enumerate(plan) if kind in kinds
        ]

    def of_x(c, kinds):
        return copies(lambda q: xg.at[c, q], c, tokens, kinds)

    def of_meta(kinds):
        return copies(lambda q: meta.at[q], pieces, 16, kinds)

    def start(group):
        for copy in group:
            copy.start()

    def await_recv(group):
        for copy in group:
            copy.wait_recv()

    def load_x(c):
        return pltpu.make_async_copy(x_hbm.at[:, pl.ds(c * width, width)], xg.at[c, 0], xsem.at[c])

    load_meta = pltpu.make_async_copy(meta_hbm, meta.at[0], xsem.at[pieces])

    def w_copy(src, slot, part):
        return pltpu.make_async_copy(src, wbuf.at[slot, :, pl.ds(part * ff, ff)], wsem.at[slot, part])

    def fetch(g):
        slot = lax.rem(g, ring)

        @pl.when(g < shared_steps)
        def _():
            rows = pl.ds(pl.multiple_of(g // 2 * width, width), width)
            for which, src in enumerate((sg, su)):

                @pl.when(lax.rem(g, 2) == which)
                def _():
                    for part in range(2):
                        w_copy(src.at[rows, pl.ds(part * ff, ff)], slot, part).start()

        @pl.when(jnp.logical_and(g >= shared_steps, g < total))
        def _():
            at = g - shared_steps
            rows = pl.ds(pl.multiple_of(at // own * width, width), width)
            for part, src in enumerate((wg, wu)):
                w_copy(src.at[lax.rem(at, own), rows], slot, part).start()

    def await_w(slot):
        for part in range(2):
            w_copy(wg.at[0, pl.ds(0, width)], slot, part).wait()

    load_meta.start()
    for c in range(pieces):
        load_x(c).start()
    for g in range(ring - 1):
        fetch(jnp.int32(g))
    greet((xn, yn, pn))
    load_meta.wait()
    start(of_meta(OWN))
    for c in range(pieces):
        load_x(c).wait()
        if c < 2:
            start(of_x(c, OWN))

    def accumulate(e, c, lhs, slot):
        for n0, n1 in spread(2 * ff):
            old = jnp.where(c == 0, 0.0, acc[e, :, n0:n1])
            acc[e, :, n0:n1] = old + dot(lhs, wbuf[slot, :, n0:n1])

    def shared(g, _):
        fetch(g + ring - 1)
        slot = lax.rem(g, ring)
        await_w(slot)
        c = g // 2
        accumulate(lax.rem(g, 2), c, xg[c, 0], slot)

        @pl.when(g == 2)
        def _():
            await_recv(of_meta(NEAR))
            start(of_meta(RELAY))

        @pl.when(g == 6)
        def _():
            await_recv(of_meta(FAR))
            start(of_meta(LAST))

        @pl.when(g == 7)
        def _():
            relay(0)
            start(of_x(2, OWN))

        return 0

    def relay(c):
        await_recv(of_x(c, NEAR))
        start(of_x(c, RELAY))

    lax.fori_loop(0, shared_steps, shared, 0)

    def out_hs(part):
        return pltpu.make_async_copy(stage.at[part], hs_out.at[:, pl.ds(part * ff, ff)], osem.at[part])

    for part in range(2):
        for n0, n1 in spread(ff):
            at = slice(part * ff + n0, part * ff + n1)
            stage[part, :, n0:n1] = (jax.nn.silu(acc[0, :, at]) * acc[1, :, at]).astype(BF16)
        out_hs(part).start()

    await_recv(of_meta(PARTNER))
    base = (me * (own * PAD)).astype(F32)
    row = lax.broadcasted_iota(jnp.int32, (PAD, tokens), 0).astype(F32)

    def out_ct(q):
        return pltpu.make_async_copy(ctst.at[lax.rem(q, 2)], ct_out.at[q], csem.at[lax.rem(q, 2)])

    def one_hot(q, _):
        @pl.when(q >= 2)
        def _():
            out_ct(q - 2).wait()

        place, gate = meta[q, 0:8] - base, meta[q, 8:16]
        for e in range(own):
            p = jnp.zeros((PAD, tokens), F32)
            c = jnp.zeros((PAD, tokens), F32)
            for j in range(6):
                hit = (place[j : j + 1] - float(e * PAD)) == row
                p = jnp.where(hit, 1.0, p)
                c = jnp.where(hit, gate[j : j + 1], c)
            pm[q, e * PAD : (e + 1) * PAD] = p.astype(BF16)
            ctst[lax.rem(q, 2), e * PAD : (e + 1) * PAD] = c.astype(BF16)
        out_ct(q).start()
        return 0

    lax.fori_loop(0, 8, one_hot, 0)
    for q in (6, 7):
        out_ct(jnp.int32(q)).wait()
    for part in range(2):
        out_hs(part).wait()

    def gather(c):
        def place_rows(q):
            rows = dot(pm[q], xg[c, q]).astype(BF16)
            for e in range(own):
                z[e, q * PAD : (q + 1) * PAD] = rows[e * PAD : (e + 1) * PAD]

        await_recv(of_x(c, FAR))
        start(of_x(c, LAST))
        for q in range(4):
            place_rows(q)
        await_recv(of_x(c, PARTNER))
        for q in range(4, 8):
            place_rows(q)

    def piece(c, _):
        relay(c + 1)

        @pl.when(c + 3 < pieces)
        def _():
            start(of_x(c + 3, OWN))

        gather(c)

        def expert(e, _):
            g = shared_steps + c * own + e
            fetch(g + ring - 1)
            slot = lax.rem(g, ring)
            await_w(slot)
            accumulate(e, c, z[e], slot)
            return 0

        return lax.fori_loop(0, own, expert, 0)

    lax.fori_loop(0, pieces - 1, piece, 0)

    last = pieces - 1
    gather(last)

    def out_h(e):
        return pltpu.make_async_copy(stage.at[lax.rem(e, 2)], h_out.at[e], osem.at[lax.rem(e, 2)])

    def finish(e, _):
        g = shared_steps + last * own + e
        fetch(g + ring - 1)
        slot = lax.rem(g, ring)
        await_w(slot)

        @pl.when(e >= 2)
        def _():
            out_h(e - 2).wait()

        lhs = z[e]
        for n0, n1 in spread(ff):
            a = acc[e, :, n0:n1] + dot(lhs, wbuf[slot, :, n0:n1])
            b = acc[e, :, ff + n0 : ff + n1] + dot(lhs, wbuf[slot, :, ff + n0 : ff + n1])
            stage[lax.rem(e, 2), :, n0:n1] = (jax.nn.silu(a) * b).astype(BF16)
        out_h(e).start()
        return 0

    lax.fori_loop(0, own, finish, 0)
    for e in (own - 2, own - 1):
        out_h(jnp.int32(e)).wait()

    def drain(c, _):
        for copy in of_x(c, range(8)):
            copy.wait_send()
        return 0

    lax.fori_loop(0, pieces, drain, 0)
    for copy in of_meta(range(8)):
        copy.wait_send()


def second_kernel(
    dims, h_hbm, hs_hbm, ct_hbm, wd, sd, y_hbm,
    h, hs, ct, wbuf, sbuf, out, keep, dsend, drecv, s1, r1, s2, r2, yst,
    lsem, wsem, ssem, ysem, send, recv,
):
    tiles, width, tokens, own, ring = dims
    me, xn, yn, pn = neighbours()
    half = tokens // 2
    low, high = pl.ds(0, half), pl.ds(half, half)

    def remote(t, kind, src, dst, device):
        return pltpu.make_async_remote_copy(
            src_ref=src, dst_ref=dst, send_sem=send.at[t, kind], recv_sem=recv.at[t, kind],
            device_id={"ep": device}, device_id_type=MESH,
        )

    def to_partner(t):
        return remote(t, 0, dsend.at[t], drecv.at[t], pn)

    def phase_one(t):
        a, b = pl.ds(0, 2), pl.ds(2, 2)
        return (
            remote(t, 1, s1.at[t, a], r1.at[t, a], xn),
            remote(t, 2, s1.at[t, b], r1.at[t, b], yn),
        )

    def phase_two(t):
        return (
            remote(t, 3, s2.at[t, 0], r2.at[t, 0], yn),
            remote(t, 4, s2.at[t, 1], r2.at[t, 1], xn),
        )

    def columns(t):
        return pl.ds(pl.multiple_of(t * width, width), width)

    def w_copy(g):
        slot = lax.rem(g, ring)
        return pltpu.make_async_copy(wd.at[lax.rem(g, own), :, columns(g // own)], wbuf.at[slot], wsem.at[slot])

    def s_copy(t):
        slot = lax.rem(t, 2)
        return pltpu.make_async_copy(sd.at[:, columns(t)], sbuf.at[slot], ssem.at[slot])

    def h_copy(e):
        return pltpu.make_async_copy(h_hbm.at[e], h.at[e], lsem.at[e])

    def y_copy(t):
        slot = lax.rem(t, 2)
        return pltpu.make_async_copy(yst.at[slot], y_hbm.at[:, columns(t)], ysem.at[slot])

    load_ct = pltpu.make_async_copy(ct_hbm, ct, lsem.at[own])
    load_hs = pltpu.make_async_copy(hs_hbm, hs, lsem.at[own + 1])

    for e in range(own):
        h_copy(e).start()
        if e < ring - 1:
            w_copy(jnp.int32(e)).start()
    load_ct.start()
    load_hs.start()
    s_copy(jnp.int32(0)).start()
    greet((xn, yn, pn))

    def compute(t):
        @pl.when(t + 1 < tiles)
        def _():
            s_copy(t + 1).start()

        def expert(e, _):
            g = t * own + e

            @pl.when(g + ring - 1 < tiles * own)
            def _():
                w_copy(g + ring - 1).start()

            @pl.when(t == 0)
            def _():
                h_copy(e).wait()

            w_copy(g).wait()
            rows = dot(h[e], wbuf[lax.rem(g, ring)]).astype(BF16)
            at = pl.ds(pl.multiple_of(e * PAD, 16), PAD)
            for q in range(8):
                out[q, at] = rows[q * PAD : (q + 1) * PAD]
            return 0

        lax.fori_loop(0, own, expert, 0)

        @pl.when(t == 0)
        def _():
            load_ct.wait()
            load_hs.wait()

        def terms(q):
            return lax.dot_general(ct[q], out[q], (((0,), (0,)), ((), ())), preferred_element_type=F32)

        for q in range(4, 8):
            dsend[t, q - 4] = terms(q).astype(BF16)
        to_partner(t).start()
        s_copy(t).wait()
        keep[t, 0] = terms(0) + dot(hs[...], sbuf[lax.rem(t, 2)])
        for q in range(1, 4):
            keep[t, q] = terms(q)

    def stage_one(t):
        to_partner(t).wait_recv()

        def both(q, rows):
            return keep[t, q, rows] + drecv[t, q, rows].astype(F32)

        s1[t, 0] = both(1, low).astype(BF16)
        s1[t, 1] = both(3, low).astype(BF16)
        s1[t, 2] = both(2, high).astype(BF16)
        s1[t, 3] = both(3, high).astype(BF16)
        for copy in phase_one(t):
            copy.start()
        keep[t, 0] = keep[t, 0] + drecv[t, 0].astype(F32)
        keep[t, 1, high] = both(1, high)
        keep[t, 2, low] = both(2, low)

    def stage_two(t):
        for copy in phase_one(t):
            copy.wait_recv()
        s2[t, 0] = (keep[t, 2, low] + r1[t, 1].astype(F32)).astype(BF16)
        s2[t, 1] = (keep[t, 1, high] + r1[t, 3].astype(F32)).astype(BF16)
        for copy in phase_two(t):
            copy.start()
        keep[t, 0, low] = keep[t, 0, low] + r1[t, 0].astype(F32)
        keep[t, 0, high] = keep[t, 0, high] + r1[t, 2].astype(F32)

    def stage_three(t):
        for copy in phase_two(t):
            copy.wait_recv()

        @pl.when(t >= 2)
        def _():
            y_copy(t - 2).wait()

        slot = lax.rem(t, 2)
        yst[slot, low] = (keep[t, 0, low] + r2[t, 0].astype(F32)).astype(BF16)
        yst[slot, high] = (keep[t, 0, high] + r2[t, 1].astype(F32)).astype(BF16)
        y_copy(t).start()

    def tile(t, _):
        @pl.when(t < tiles)
        def _():
            compute(t)
            stage_one(t)

        @pl.when(jnp.logical_and(t >= 1, t <= tiles))
        def _():
            stage_two(t - 1)

        @pl.when(t >= 2)
        def _():
            stage_three(t - 2)

        return 0

    lax.fori_loop(0, tiles + 2, tile, 0)
    for t in (tiles - 2, tiles - 1):
        y_copy(jnp.int32(t)).wait()

    def drain(t, _):
        for copy in (to_partner(t), *phase_one(t), *phase_two(t)):
            copy.wait_send()
        return 0

    lax.fori_loop(0, tiles, drain, 0)


def solution(mesh):
    members = mesh.shape["ep"]

    def body(x, expert, slot, gate, w_gate, w_up, w_down, s_gate, s_up, s_down):
        tokens, top = expert.shape[2:]
        own, d, ff = w_gate.shape
        slots = 5 * tokens * top // (4 * own * members)
        x, expert, slot, gate = x[0, 0], expert[0, 0], slot[0, 0], gate[0, 0]
        place = jnp.where(slot < slots, expert * PAD + slot, -1).astype(F32)
        fill = ((0, 8 - top), (0, 0))
        meta = jnp.concatenate([jnp.pad(place.T, fill, constant_values=-1.0), jnp.pad(gate.T, fill)])

        hbm = pl.BlockSpec(memory_space=pl.ANY)
        dma = pltpu.SemaphoreType.DMA
        pieces, ring = 8, 4
        width = d // pieces
        rows = own * PAD
        h, hs, ct = pl.pallas_call(
            functools.partial(first_kernel, (pieces, width, tokens, ff, own, ring)),
            out_shape=(
                jax.ShapeDtypeStruct((own, rows, ff), BF16),
                jax.ShapeDtypeStruct((tokens, 2 * ff), BF16),
                jax.ShapeDtypeStruct((8, rows, tokens), BF16),
            ),
            in_specs=[hbm] * 6,
            out_specs=(hbm,) * 3,
            scratch_shapes=[
                pltpu.VMEM((pieces, 8, tokens, width), BF16),
                pltpu.VMEM((8, 16, tokens), F32),
                pltpu.VMEM((own, rows, 2 * ff), F32),
                pltpu.VMEM((ring, width, 2 * ff), BF16),
                pltpu.VMEM((own, rows, width), BF16),
                pltpu.VMEM((8, rows, tokens), BF16),
                pltpu.VMEM((2, rows, ff), BF16),
                pltpu.VMEM((2, rows, tokens), BF16),
                dma((pieces + 1,)),
                dma((ring, 2)),
                dma((2,)),
                dma((2,)),
                dma((pieces + 1, 8)),
                dma((pieces + 1, 8)),
            ],
            compiler_params=pltpu.CompilerParams(
                collective_id=0, has_side_effects=True, vmem_limit_bytes=VMEM_BYTES
            ),
            name="dispatch_up",
        )(x, meta, w_gate, w_up, s_gate, s_up)

        tiles, ring = 8, 6
        width = d // tiles
        y = pl.pallas_call(
            functools.partial(second_kernel, (tiles, width, tokens, own, ring)),
            out_shape=jax.ShapeDtypeStruct((tokens, d), BF16),
            in_specs=[hbm] * 5,
            out_specs=hbm,
            scratch_shapes=[
                pltpu.VMEM((own, rows, ff), BF16),
                pltpu.VMEM((tokens, 2 * ff), BF16),
                pltpu.VMEM((8, rows, tokens), BF16),
                pltpu.VMEM((ring, ff, width), BF16),
                pltpu.VMEM((2, 2 * ff, width), BF16),
                pltpu.VMEM((8, rows, width), BF16),
                pltpu.VMEM((tiles, 4, tokens, width), F32),
                pltpu.VMEM((tiles, 4, tokens, width), BF16),
                pltpu.VMEM((tiles, 4, tokens, width), BF16),
                pltpu.VMEM((tiles, 4, tokens // 2, width), BF16),
                pltpu.VMEM((tiles, 4, tokens // 2, width), BF16),
                pltpu.VMEM((tiles, 2, tokens // 2, width), BF16),
                pltpu.VMEM((tiles, 2, tokens // 2, width), BF16),
                pltpu.VMEM((2, tokens, width), BF16),
                dma((own + 2,)),
                dma((ring,)),
                dma((2,)),
                dma((2,)),
                dma((tiles, 5)),
                dma((tiles, 5)),
            ],
            compiler_params=pltpu.CompilerParams(
                collective_id=1, has_side_effects=True, vmem_limit_bytes=VMEM_BYTES
            ),
            name="down_combine",
        )(h, hs, ct, w_down, s_down)
        return y[None, None]

    tok, exp, rep = P("dp", "ep"), P("ep"), P()
    return jax.shard_map(
        body,
        mesh=mesh,
        in_specs=(tok,) * 4 + (exp,) * 3 + (rep,) * 3,
        out_specs=tok,
        check_vma=False,
    )
```

profile of v0, /device:TPU:0, one launch (start us, length us, event | category | flops | bytes accessed | tf_op | source)
XLA Modules:
  0.0 187.9 jit_solution(6057461340274960740)
XLA Ops:
  0.0 0.7 fusion.2
  0.7 0.7 copy.29
  1.4 0.6 select_maximum_fusion.meta_hbm
  2.0 106.7 %dispatch_up.1 = (bf16[8,384,1408]{2,1,0:T(8,128)(2,1)}, bf16[384,2816]{1,0:T(8,128)(2,1)}, bf16[8,384,384]{2,1,0:T(8,128)(2,1)}) custom-call(bf16[384,2048]{1,0:T(8,128)(2,1)} %bitcast.12, f32[16,384]{1,0:T(8,128)} %select_maximum_fusion.meta_hbm, bf16[8,2048,1408]{2,1,0:T(8,128)(2,1)} %wg.1, bf16[8,2048,1408]{2,1,0:T(8,128)(2,1)} %wu.1, ...), custom_call_target="tpu_custom_call" | custom-call | tf_op jit(solution)/shard_map/dispatch_up/pallas_call | solution.py:458
  108.7 76.4 %down_combine.1 = bf16[384,2048]{1,0:T(8,128)(2,1)} custom-call(bf16[8,384,1408]{2,1,0:T(8,128)(2,1)} %get-tuple-element.8.h_hbm, bf16[384,2816]{1,0:T(8,128)(2,1)} %get-tuple-element.9.hs_hbm, bf16[8,384,384]{2,1,0:T(8,128)(2,1)} %get-tuple-element.10.ct_hbm, bf16[8,1408,2048]{2,1,0:T(8,128)(2,1)} %wd.1, bf16[2816,2048]{1,0:T(8,128)(2,1)} %sd.1), custom_call_target="tpu_custom_call" | custom-call | tf_op jit(solution)/shard_map/down_combine/pallas_call | solution.py:491
  185.1 2.7 %copy.31 = bf16[1,1,384,2048]{3,2,1,0:T(8,128)(2,1)} copy(bf16[1,1,384,2048]{3,2,1,0:T(8,128)(2,1)} %bitcast.11) | data formatting | bytes 3145728
where the time goes:
time: 188 us
  Pallas kernels  183 us (97%)
  local copies, waits for them, and re-layouts  3.43 us (2%)
    pallas_call x1, Pallas kernels, body(): pl.pallas_call(functools.partial(first_kernel, (pieces, width, tokens, ff...  107 us
    pallas_call x1, Pallas kernels, body(): pl.pallas_call(functools.partial(second_kernel, (tiles, width, tokens, ow...  76.4 us

commit v1 on v0

--- a/solution.py
+++ b/solution.py
@@ -10,6 +10,7 @@
 MESH = pl.DeviceIdType.MESH
 F32, BF16 = jnp.float32, jnp.bfloat16
 VMEM_BYTES = 67043328
+GROUP = 4
 PAD = 48
 OWN, NEAR, FAR, RELAY, LAST, PARTNER = (0, 1, 2), (0, 1), (3, 4), (3, 4, 5, 6), (7,), (2, 5, 6, 7)
 
@@ -110,7 +111,7 @@
     load_meta.start()
     for c in range(pieces):
         load_x(c).start()
-    for g in range(ring - 1):
+    for g in range(GROUP):
         fetch(jnp.int32(g))
     greet((xn, yn, pn))
     load_meta.wait()
@@ -120,40 +121,46 @@
         if c < 2:
             start(of_x(c, OWN))
 
-    def accumulate(e, c, lhs, slot):
-        for n0, n1 in spread(2 * ff):
-            old = jnp.where(c == 0, 0.0, acc[e, :, n0:n1])
-            acc[e, :, n0:n1] = old + dot(lhs, wbuf[slot, :, n0:n1])
-
-    def shared(g, _):
-        fetch(g + ring - 1)
-        slot = lax.rem(g, ring)
-        await_w(slot)
-        c = g // 2
-        accumulate(lax.rem(g, 2), c, xg[c, 0], slot)
-
-        @pl.when(g == 2)
-        def _():
-            await_recv(of_meta(NEAR))
-            start(of_meta(RELAY))
-
-        @pl.when(g == 6)
-        def _():
-            await_recv(of_meta(FAR))
-            start(of_meta(LAST))
-
-        @pl.when(g == 7)
-        def _():
-            relay(0)
-            start(of_x(2, OWN))
-
+    def take(group):
+        for i in range(GROUP):
+            fetch((group + 1) * GROUP + i)
+        slots = [lax.rem(group * GROUP + i, ring) for i in range(GROUP)]
+        for slot in slots:
+            await_w(slot)
+        return slots
+
+    def shared(p, _, new):
+        slots = take(p)
+        for which in range(2):
+            for n0, n1 in spread(2 * ff):
+                terms = sum(dot(xg[2 * p + i, 0], wbuf[slots[2 * i + which], :, n0:n1]) for i in range(2))
+                acc[which, :, n0:n1] = terms if new else acc[which, :, n0:n1] + terms
         return 0
 
     def relay(c):
         await_recv(of_x(c, NEAR))
         start(of_x(c, RELAY))
 
-    lax.fori_loop(0, shared_steps, shared, 0)
+    shared(0, 0, True)
+    await_recv(of_meta(NEAR))
+    start(of_meta(RELAY))
+
+    def shared_rest(p, _):
+        shared(p, 0, False)
+
+        @pl.when(p == 1)
+        def _():
+            await_recv(of_meta(FAR))
+            start(of_meta(LAST))
+
+        @pl.when(p == 2)
+        def _():
+            relay(0)
+            start(of_x(2, OWN))
+
+        return 0
+
+    lax.fori_loop(1, shared_steps // GROUP, shared_rest, 0)
 
     def out_hs(part):
         return pltpu.make_async_copy(stage.at[part], hs_out.at[:, pl.ds(part * ff, ff)], osem.at[part])
@@ -209,7 +216,7 @@
         for q in range(4, 8):
             place_rows(q)
 
-    def piece(c, _):
+    def piece(c, _, new):
         relay(c + 1)
 
         @pl.when(c + 3 < pieces)
@@ -218,17 +225,20 @@
 
         gather(c)
 
-        def expert(e, _):
-            g = shared_steps + c * own + e
-            fetch(g + ring - 1)
-            slot = lax.rem(g, ring)
-            await_w(slot)
-            accumulate(e, c, z[e], slot)
+        def experts(i, _):
+            slots = take((shared_steps + c * own) // GROUP + i)
+            for j, slot in enumerate(slots):
+                e = i * GROUP + j
+                lhs = z[e]
+                for n0, n1 in spread(2 * ff):
+                    term = dot(lhs, wbuf[slot, :, n0:n1])
+                    acc[e, :, n0:n1] = term if new else acc[e, :, n0:n1] + term
             return 0
 
-        return lax.fori_loop(0, own, expert, 0)
-
-    lax.fori_loop(0, pieces - 1, piece, 0)
+        return lax.fori_loop(0, own // GROUP, experts, 0)
+
+    piece(jnp.int32(0), 0, True)
+    lax.fori_loop(1, pieces - 1, functools.partial(piece, new=False), 0)
 
     last = pieces - 1
     gather(last)
@@ -236,25 +246,27 @@
     def out_h(e):
         return pltpu.make_async_copy(stage.at[lax.rem(e, 2)], h_out.at[e], osem.at[lax.rem(e, 2)])
 
-    def finish(e, _):
-        g = shared_steps + last * own + e
-        fetch(g + ring - 1)
-        slot = lax.rem(g, ring)
-        await_w(slot)
-
-        @pl.when(e >= 2)
-        def _():
-            out_h(e - 2).wait()
-
-        lhs = z[e]
-        for n0, n1 in spread(ff):
-            a = acc[e, :, n0:n1] + dot(lhs, wbuf[slot, :, n0:n1])
-            b = acc[e, :, ff + n0 : ff + n1] + dot(lhs, wbuf[slot, :, ff + n0 : ff + n1])
-            stage[lax.rem(e, 2), :, n0:n1] = (jax.nn.silu(a) * b).astype(BF16)
-        out_h(e).start()
-        return 0
-
-    lax.fori_loop(0, own, finish, 0)
+    def finish(i, _):
+        slots = take((shared_steps + last * own) // GROUP + i)
+        for j, slot in enumerate(slots):
+            e = i * GROUP + j
+            if j >= 2:
+                out_h(e - 2).wait()
+            else:
+
+                @pl.when(i > 0)
+                def _():
+                    out_h(e - 2).wait()
+
+            lhs = z[e]
+            for n0, n1 in spread(ff):
+                a = acc[e, :, n0:n1] + dot(lhs, wbuf[slot, :, n0:n1])
+                b = acc[e, :, ff + n0 : ff + n1] + dot(lhs, wbuf[slot, :, ff + n0 : ff + n1])
+                stage[j % 2, :, n0:n1] = (jax.nn.silu(a) * b).astype(BF16)
+            out_h(e).start()
+        return 0
+
+    lax.fori_loop(0, own // GROUP, finish, 0)
     for e in (own - 2, own - 1):
         out_h(jnp.int32(e)).wait()
 
@@ -323,7 +335,7 @@
 
     for e in range(own):
         h_copy(e).start()
-        if e < ring - 1:
+        if e < GROUP:
             w_copy(jnp.int32(e)).start()
     load_ct.start()
     load_hs.start()
@@ -335,25 +347,30 @@
         def _():
             s_copy(t + 1).start()
 
-        def expert(e, _):
-            g = t * own + e
-
-            @pl.when(g + ring - 1 < tiles * own)
+        def experts(i, _):
+            g = t * own + i * GROUP
+
+            @pl.when(g + GROUP < tiles * own)
             def _():
-                w_copy(g + ring - 1).start()
+                for j in range(GROUP):
+                    w_copy(g + GROUP + j).start()
 
             @pl.when(t == 0)
             def _():
-                h_copy(e).wait()
-
-            w_copy(g).wait()
-            rows = dot(h[e], wbuf[lax.rem(g, ring)]).astype(BF16)
-            at = pl.ds(pl.multiple_of(e * PAD, 16), PAD)
-            for q in range(8):
-                out[q, at] = rows[q * PAD : (q + 1) * PAD]
+                for j in range(GROUP):
+                    h_copy(i * GROUP + j).wait()
+
+            for j in range(GROUP):
+                w_copy(g + j).wait()
+            for j in range(GROUP):
+                e = i * GROUP + j
+                rows = dot(h[e], wbuf[lax.rem(g + j, ring)]).astype(BF16)
+                at = pl.ds(pl.multiple_of(e * PAD, 16), PAD)
+                for q in range(8):
+                    out[q, at] = rows[q * PAD : (q + 1) * PAD]
             return 0
 
-        lax.fori_loop(0, own, expert, 0)
+        lax.fori_loop(0, own // GROUP, experts, 0)
 
         @pl.when(t == 0)
         def _():
@@ -452,7 +469,7 @@
 
         hbm = pl.BlockSpec(memory_space=pl.ANY)
         dma = pltpu.SemaphoreType.DMA
-        pieces, ring = 8, 4
+        pieces, ring = 8, 2 * GROUP
         width = d // pieces
         rows = own * PAD
         h, hs, ct = pl.pallas_call(
@@ -486,7 +503,7 @@
             name="dispatch_up",
         )(x, meta, w_gate, w_up, s_gate, s_up)
 
-        tiles, ring = 8, 6
+        tiles, ring = 8, 2 * GROUP
         width = d // tiles
         y = pl.pallas_call(
             functools.partial(second_kernel, (tiles, width, tokens, own, ring)),

time: 188 us -> 171 us (0.910)
  Pallas kernels: 183 us -> 166 us
    pallas_call x1, Pallas kernels: 107 us -> 90.3 us  [body(): pl.pallas_call(functools.partial(first_kernel, (pieces, width, tokens, ff...]
where the time goes in v1:
time: 171 us
  Pallas kernels  166 us (97%)
  local copies, waits for them, and re-layouts  3.43 us (2%)
    pallas_call x1, Pallas kernels, body(): pl.pallas_call(functools.partial(first_kernel, (pieces, width, tokens, ff...  90.3 us
    pallas_call x1, Pallas kernels, body(): pl.pallas_call(functools.partial(second_kernel, (tiles, width, tokens, ow...  75.5 us
    unnamed x2, local copies, waits for them, and re-layouts  3.43 us

profile of v1, /device:TPU:0, one launch (start us, length us, event | category | flops | bytes accessed | tf_op | source)
XLA Modules:
  0.0 170.6 jit_solution(9340216908787130258)
XLA Ops:
  0.0 0.7 fusion.2
  0.7 0.7 copy.29
  1.4 0.6 select_maximum_fusion.meta_hbm
  2.0 90.3 %dispatch_up.1 = (bf16[8,384,1408]{2,1,0:T(8,128)(2,1)}, bf16[384,2816]{1,0:T(8,128)(2,1)}, bf16[8,384,384]{2,1,0:T(8,128)(2,1)}) custom-call(bf16[384,2048]{1,0:T(8,128)(2,1)} %bitcast.12, f32[16,384]{1,0:T(8,128)} %select_maximum_fusion.meta_hbm, bf16[8,2048,1408]{2,1,0:T(8,128)(2,1)} %wg.1, bf16[8,2048,1408]{2,1,0:T(8,128)(2,1)} %wu.1, ...), custom_call_target="tpu_custom_call" | custom-call | tf_op jit(solution)/shard_map/dispatch_up/pallas_call | solution.py:475
  92.4 75.5 %down_combine.1 = bf16[384,2048]{1,0:T(8,128)(2,1)} custom-call(bf16[8,384,1408]{2,1,0:T(8,128)(2,1)} %get-tuple-element.8.h_hbm, bf16[384,2816]{1,0:T(8,128)(2,1)} %get-tuple-element.9.hs_hbm, bf16[8,384,384]{2,1,0:T(8,128)(2,1)} %get-tuple-element.10.ct_hbm, bf16[8,1408,2048]{2,1,0:T(8,128)(2,1)} %wd.1, bf16[2816,2048]{1,0:T(8,128)(2,1)} %sd.1), custom_call_target="tpu_custom_call" | custom-call | tf_op jit(solution)/shard_map/down_combine/pallas_call | solution.py:508
  167.9 2.7 %copy.31 = bf16[1,1,384,2048]{3,2,1,0:T(8,128)(2,1)} copy(bf16[1,1,384,2048]{3,2,1,0:T(8,128)(2,1)} %bitcast.11) | data formatting | bytes 3145728

commit v2 on v1

--- a/solution.py
+++ b/solution.py
@@ -10,7 +10,7 @@
 MESH = pl.DeviceIdType.MESH
 F32, BF16 = jnp.float32, jnp.bfloat16
 VMEM_BYTES = 67043328
-GROUP = 4
+GROUP, BATCH = 4, 4
 PAD = 48
 OWN, NEAR, FAR, RELAY, LAST, PARTNER = (0, 1, 2), (0, 1), (3, 4), (3, 4, 5, 6), (7,), (2, 5, 6, 7)
 
@@ -111,7 +111,7 @@
     load_meta.start()
     for c in range(pieces):
         load_x(c).start()
-    for g in range(GROUP):
+    for g in range(ring - GROUP):
         fetch(jnp.int32(g))
     greet((xn, yn, pn))
     load_meta.wait()
@@ -123,14 +123,14 @@
 
     def take(group):
         for i in range(GROUP):
-            fetch((group + 1) * GROUP + i)
+            fetch(group * GROUP + ring - GROUP + i)
         slots = [lax.rem(group * GROUP + i, ring) for i in range(GROUP)]
         for slot in slots:
             await_w(slot)
         return slots
 
     def shared(p, _, new):
-        slots = take(p)
+        slots = [slot for i in range(4 // GROUP) for slot in take(p * (4 // GROUP) + i)]
         for which in range(2):
             for n0, n1 in spread(2 * ff):
                 terms = sum(dot(xg[2 * p + i, 0], wbuf[slots[2 * i + which], :, n0:n1]) for i in range(2))
@@ -160,7 +160,7 @@
 
         return 0
 
-    lax.fori_loop(1, shared_steps // GROUP, shared_rest, 0)
+    lax.fori_loop(1, shared_steps // 4, shared_rest, 0)
 
     def out_hs(part):
         return pltpu.make_async_copy(stage.at[part], hs_out.at[:, pl.ds(part * ff, ff)], osem.at[part])
@@ -208,24 +208,28 @@
             for e in range(own):
                 z[e, q * PAD : (q + 1) * PAD] = rows[e * PAD : (e + 1) * PAD]
 
+        await_recv(of_x(c, PARTNER))
+        for q in range(8):
+            place_rows(q)
+
+    def pass_on(c):
+        @pl.when(c + 1 < pieces)
+        def _():
+            relay(c + 1)
+
+        @pl.when(c + 3 < pieces)
+        def _():
+            start(of_x(c + 3, OWN))
+
         await_recv(of_x(c, FAR))
         start(of_x(c, LAST))
-        for q in range(4):
-            place_rows(q)
-        await_recv(of_x(c, PARTNER))
-        for q in range(4, 8):
-            place_rows(q)
 
     def piece(c, _, new):
-        relay(c + 1)
-
-        @pl.when(c + 3 < pieces)
-        def _():
-            start(of_x(c + 3, OWN))
-
-        gather(c)
-
         def experts(i, _):
+            @pl.when(i == 1)
+            def _():
+                pass_on(c + 1)
+
             slots = take((shared_steps + c * own) // GROUP + i)
             for j, slot in enumerate(slots):
                 e = i * GROUP + j
@@ -235,13 +239,16 @@
                     acc[e, :, n0:n1] = term if new else acc[e, :, n0:n1] + term
             return 0
 
-        return lax.fori_loop(0, own // GROUP, experts, 0)
-
+        lax.fori_loop(0, own // GROUP, experts, 0)
+        gather(c + 1)
+        return 0
+
+    pass_on(jnp.int32(0))
+    gather(0)
     piece(jnp.int32(0), 0, True)
     lax.fori_loop(1, pieces - 1, functools.partial(piece, new=False), 0)
 
     last = pieces - 1
-    gather(last)
 
     def out_h(e):
         return pltpu.make_async_copy(stage.at[lax.rem(e, 2)], h_out.at[e], osem.at[lax.rem(e, 2)])
@@ -335,7 +342,7 @@
 
     for e in range(own):
         h_copy(e).start()
-        if e < GROUP:
+        if e < ring - BATCH:
             w_copy(jnp.int32(e)).start()
     load_ct.start()
     load_hs.start()
@@ -348,29 +355,37 @@
             s_copy(t + 1).start()
 
         def experts(i, _):
-            g = t * own + i * GROUP
-
-            @pl.when(g + GROUP < tiles * own)
+            @pl.when(jnp.logical_and(i == 1, t >= 1))
             def _():
-                for j in range(GROUP):
-                    w_copy(g + GROUP + j).start()
+                stage_one(t - 1)
+
+            g = t * own + i * BATCH
+
+            @pl.when(g + ring - BATCH < tiles * own)
+            def _():
+                for j in range(BATCH):
+                    w_copy(g + ring - BATCH + j).start()
 
             @pl.when(t == 0)
             def _():
-                for j in range(GROUP):
-                    h_copy(i * GROUP + j).wait()
-
-            for j in range(GROUP):
+                for j in range(BATCH):
+                    h_copy(i * BATCH + j).wait()
+
+            for j in range(BATCH):
                 w_copy(g + j).wait()
-            for j in range(GROUP):
-                e = i * GROUP + j
+            for j in range(BATCH):
+                e = i * BATCH + j
                 rows = dot(h[e], wbuf[lax.rem(g + j, ring)]).astype(BF16)
                 at = pl.ds(pl.multiple_of(e * PAD, 16), PAD)
                 for q in range(8):
                     out[q, at] = rows[q * PAD : (q + 1) * PAD]
             return 0
 
-        lax.fori_loop(0, own // GROUP, experts, 0)
+        lax.fori_loop(0, own // BATCH, experts, 0)
+
+        @pl.when(t >= 2)
+        def _():
+            stage_two(t - 2)
 
         @pl.when(t == 0)
         def _():
@@ -431,19 +446,22 @@
         @pl.when(t < tiles)
         def _():
             compute(t)
-            stage_one(t)
-
-        @pl.when(jnp.logical_and(t >= 1, t <= tiles))
-        def _():
-            stage_two(t - 1)
-
-        @pl.when(t >= 2)
-        def _():
-            stage_three(t - 2)
-
-        return 0
-
-    lax.fori_loop(0, tiles + 2, tile, 0)
+
+        @pl.when(t == tiles)
+        def _():
+            stage_one(t - 1)
+
+        @pl.when(jnp.logical_and(t >= tiles, t <= tiles + 1))
+        def _():
+            stage_two(t - 2)
+
+        @pl.when(t >= 3)
+        def _():
+            stage_three(t - 3)
+
+        return 0
+
+    lax.fori_loop(0, tiles + 3, tile, 0)
     for t in (tiles - 2, tiles - 1):
         y_copy(jnp.int32(t)).wait()
 
@@ -469,7 +487,7 @@
 
         hbm = pl.BlockSpec(memory_space=pl.ANY)
         dma = pltpu.SemaphoreType.DMA
-        pieces, ring = 8, 2 * GROUP
+        pieces, ring = 8, 8
         width = d // pieces
         rows = own * PAD
         h, hs, ct = pl.pallas_call(
@@ -503,7 +521,7 @@
             name="dispatch_up",
         )(x, meta, w_gate, w_up, s_gate, s_up)
 
-        tiles, ring = 8, 2 * GROUP
+        tiles, ring = 8, 12
         width = d // tiles
         y = pl.pallas_call(
             functools.partial(second_kernel, (tiles, width, tokens, own, ring)),

time: 171 us -> 153 us (0.89)
  Pallas kernels: 166 us -> 148 us
    pallas_call x1, Pallas kernels: 90.3 us -> 80.6 us  [body(): pl.pallas_call(functools.partial(first_kernel, (pieces, width, tokens, ff...]
    pallas_call x1, Pallas kernels: 75.5 us -> 67.6 us  [body(): pl.pallas_call(functools.partial(second_kernel, (tiles, width, tokens, ow...]
where the time goes in v2:
time: 153 us
  Pallas kernels  148 us (97%)
  local copies, waits for them, and re-layouts  3.43 us (2%)
    pallas_call x1, Pallas kernels, body(): pl.pallas_call(functools.partial(first_kernel, (pieces, width, tokens, ff...  80.6 us
    pallas_call x1, Pallas kernels, body(): pl.pallas_call(functools.partial(second_kernel, (tiles, width, tokens, ow...  67.6 us
    unnamed x2, local copies, waits for them, and re-layouts  3.43 us

profile of v2, /device:TPU:0, one launch (start us, length us, event | category | flops | bytes accessed | tf_op | source)
XLA Modules:
  0.0 152.9 jit_solution(2862145494250350251)
XLA Ops:
  0.0 0.7 fusion.2
  0.7 0.7 copy.29
  1.4 0.6 select_maximum_fusion.meta_hbm
  2.0 80.6 %dispatch_up.1 = (bf16[8,384,1408]{2,1,0:T(8,128)(2,1)}, bf16[384,2816]{1,0:T(8,128)(2,1)}, bf16[8,384,384]{2,1,0:T(8,128)(2,1)}) custom-call(bf16[384,2048]{1,0:T(8,128)(2,1)} %bitcast.12, f32[16,384]{1,0:T(8,128)} %select_maximum_fusion.meta_hbm, bf16[8,2048,1408]{2,1,0:T(8,128)(2,1)} %wg.1, bf16[8,2048,1408]{2,1,0:T(8,128)(2,1)} %wu.1, ...), custom_call_target="tpu_custom_call" | custom-call | tf_op jit(solution)/shard_map/dispatch_up/pallas_call | solution.py:493
  82.6 67.6 %down_combine.1 = bf16[384,2048]{1,0:T(8,128)(2,1)} custom-call(bf16[8,384,1408]{2,1,0:T(8,128)(2,1)} %get-tuple-element.8.h_hbm, bf16[384,2816]{1,0:T(8,128)(2,1)} %get-tuple-element.9.hs_hbm, bf16[8,384,384]{2,1,0:T(8,128)(2,1)} %get-tuple-element.10.ct_hbm, bf16[8,1408,2048]{2,1,0:T(8,128)(2,1)} %wd.1, bf16[2816,2048]{1,0:T(8,128)(2,1)} %sd.1), custom_call_target="tpu_custom_call" | custom-call | tf_op jit(solution)/shard_map/down_combine/pallas_call | solution.py:526
  150.2 2.7 %copy.31 = bf16[1,1,384,2048]{3,2,1,0:T(8,128)(2,1)} copy(bf16[1,1,384,2048]{3,2,1,0:T(8,128)(2,1)} %bitcast.11) | data formatting | bytes 3145728

commit v3 on v2

--- a/solution.py
+++ b/solution.py
@@ -37,14 +37,14 @@
 
 
 def first_kernel(
-    dims, x_hbm, meta_hbm, wg, wu, sg, su, h_out, hs_out, ct_out,
+    dims, x_hbm, meta_hbm, wg, wu, h_out, ct_out,
     xg, meta, acc, wbuf, z, pm, stage, ctst, xsem, wsem, osem, csem, send, recv,
 ):
     pieces, width, tokens, ff, own, ring = dims
     me, xn, yn, pn = neighbours()
-    half = tokens // 2
-    shared_steps = 2 * pieces
-    total = shared_steps + pieces * own
+    dn = xn + yn - me
+    others = [xn, yn, dn] + [device + pn - me for device in (me, xn, yn, dn)]
+    total = pieces * own
 
     def copies(ref, piece, rows, kinds):
         mid = rows // 2
@@ -65,8 +65,14 @@
     def of_x(c, kinds):
         return copies(lambda q: xg.at[c, q], c, tokens, kinds)
 
-    def of_meta(kinds):
-        return copies(lambda q: meta.at[q], pieces, 16, kinds)
+    def of_meta():
+        return [
+            pltpu.make_async_remote_copy(
+                src_ref=meta.at[0], dst_ref=meta.at[q + 1], send_sem=send.at[pieces, q], recv_sem=recv.at[pieces, q],
+                device_id={"ep": device}, device_id_type=MESH,
+            )
+            for q, device in enumerate(others)
+        ]
 
     def start(group):
         for copy in group:
@@ -87,22 +93,11 @@
     def fetch(g):
         slot = lax.rem(g, ring)
 
-        @pl.when(g < shared_steps)
-        def _():
-            rows = pl.ds(pl.multiple_of(g // 2 * width, width), width)
-            for which, src in enumerate((sg, su)):
-
-                @pl.when(lax.rem(g, 2) == which)
-                def _():
-                    for part in range(2):
-                        w_copy(src.at[rows, pl.ds(part * ff, ff)], slot, part).start()
-
-        @pl.when(jnp.logical_and(g >= shared_steps, g < total))
-        def _():
-            at = g - shared_steps
-            rows = pl.ds(pl.multiple_of(at // own * width, width), width)
+        @pl.when(g < total)
+        def _():
+            rows = pl.ds(pl.multiple_of(g // own * width, width), width)
             for part, src in enumerate((wg, wu)):
-                w_copy(src.at[lax.rem(at, own), rows], slot, part).start()
+                w_copy(src.at[lax.rem(g, own), rows], slot, part).start()
 
     def await_w(slot):
         for part in range(2):
@@ -111,15 +106,15 @@
     load_meta.start()
     for c in range(pieces):
         load_x(c).start()
+    greet(others)
+    load_meta.wait()
+    start(of_meta())
+    load_x(0).wait()
+    start(of_x(0, OWN))
     for g in range(ring - GROUP):
         fetch(jnp.int32(g))
-    greet((xn, yn, pn))
-    load_meta.wait()
-    start(of_meta(OWN))
-    for c in range(pieces):
+    for c in range(1, pieces):
         load_x(c).wait()
-        if c < 2:
-            start(of_x(c, OWN))
 
     def take(group):
         for i in range(GROUP):
@@ -129,49 +124,11 @@
             await_w(slot)
         return slots
 
-    def shared(p, _, new):
-        slots = [slot for i in range(4 // GROUP) for slot in take(p * (4 // GROUP) + i)]
-        for which in range(2):
-            for n0, n1 in spread(2 * ff):
-                terms = sum(dot(xg[2 * p + i, 0], wbuf[slots[2 * i + which], :, n0:n1]) for i in range(2))
-                acc[which, :, n0:n1] = terms if new else acc[which, :, n0:n1] + terms
-        return 0
-
     def relay(c):
         await_recv(of_x(c, NEAR))
         start(of_x(c, RELAY))
 
-    shared(0, 0, True)
-    await_recv(of_meta(NEAR))
-    start(of_meta(RELAY))
-
-    def shared_rest(p, _):
-        shared(p, 0, False)
-
-        @pl.when(p == 1)
-        def _():
-            await_recv(of_meta(FAR))
-            start(of_meta(LAST))
-
-        @pl.when(p == 2)
-        def _():
-            relay(0)
-            start(of_x(2, OWN))
-
-        return 0
-
-    lax.fori_loop(1, shared_steps // 4, shared_rest, 0)
-
-    def out_hs(part):
-        return pltpu.make_async_copy(stage.at[part], hs_out.at[:, pl.ds(part * ff, ff)], osem.at[part])
-
-    for part in range(2):
-        for n0, n1 in spread(ff):
-            at = slice(part * ff + n0, part * ff + n1)
-            stage[part, :, n0:n1] = (jax.nn.silu(acc[0, :, at]) * acc[1, :, at]).astype(BF16)
-        out_hs(part).start()
-
-    await_recv(of_meta(PARTNER))
+    await_recv(of_meta())
     base = (me * (own * PAD)).astype(F32)
     row = lax.broadcasted_iota(jnp.int32, (PAD, tokens), 0).astype(F32)
 
@@ -199,8 +156,6 @@
     lax.fori_loop(0, 8, one_hot, 0)
     for q in (6, 7):
         out_ct(jnp.int32(q)).wait()
-    for part in range(2):
-        out_hs(part).wait()
 
     def gather(c):
         def place_rows(q):
@@ -228,9 +183,13 @@
         def experts(i, _):
             @pl.when(i == 1)
             def _():
-                pass_on(c + 1)
-
-            slots = take((shared_steps + c * own) // GROUP + i)
+                if new:
+                    relay(1)
+                    start(of_x(3, OWN))
+                else:
+                    pass_on(c + 1)
+
+            slots = take(c * own // GROUP + i)
             for j, slot in enumerate(slots):
                 e = i * GROUP + j
                 lhs = z[e]
@@ -240,10 +199,16 @@
             return 0
 
         lax.fori_loop(0, own // GROUP, experts, 0)
+        if new:
+            pass_on(c + 1)
         gather(c + 1)
         return 0
 
-    pass_on(jnp.int32(0))
+    relay(0)
+    for c in (1, 2):
+        start(of_x(c, OWN))
+    await_recv(of_x(0, FAR))
+    start(of_x(0, LAST))
     gather(0)
     piece(jnp.int32(0), 0, True)
     lax.fori_loop(1, pieces - 1, functools.partial(piece, new=False), 0)
@@ -254,7 +219,7 @@
         return pltpu.make_async_copy(stage.at[lax.rem(e, 2)], h_out.at[e], osem.at[lax.rem(e, 2)])
 
     def finish(i, _):
-        slots = take((shared_steps + last * own) // GROUP + i)
+        slots = take(last * own // GROUP + i)
         for j, slot in enumerate(slots):
             e = i * GROUP + j
             if j >= 2:
@@ -283,19 +248,20 @@
         return 0
 
     lax.fori_loop(0, pieces, drain, 0)
-    for copy in of_meta(range(8)):
+    for copy in of_meta():
         copy.wait_send()
 
 
 def second_kernel(
-    dims, h_hbm, hs_hbm, ct_hbm, wd, sd, y_hbm,
-    h, hs, ct, wbuf, sbuf, out, keep, dsend, drecv, s1, r1, s2, r2, yst,
-    lsem, wsem, ssem, ysem, send, recv,
+    dims, h_hbm, ct_hbm, x_hbm, wd, sg, su, sd, y_hbm,
+    h, ct, x, hs, wbuf, ubuf, sbuf, out, keep, dsend, drecv, s1, r1, s2, r2, yst,
+    lsem, wsem, usem, ssem, ysem, send, recv,
 ):
     tiles, width, tokens, own, ring = dims
     me, xn, yn, pn = neighbours()
     half = tokens // 2
     low, high = pl.ds(0, half), pl.ds(half, half)
+    slices = hs.shape[1] // width
 
     def remote(t, kind, src, dst, device):
         return pltpu.make_async_remote_copy(
@@ -304,7 +270,7 @@
         )
 
     def to_partner(t):
-        return remote(t, 0, dsend.at[t], drecv.at[t], pn)
+        return remote(t, 0, dsend.at[lax.rem(t, 3)], drecv.at[t], pn)
 
     def phase_one(t):
         a, b = pl.ds(0, 2), pl.ds(2, 2)
@@ -330,6 +296,13 @@
         slot = lax.rem(t, 2)
         return pltpu.make_async_copy(sd.at[:, columns(t)], sbuf.at[slot], ssem.at[slot])
 
+    def u_copies(j):
+        slot = lax.rem(j, 2)
+        return [
+            pltpu.make_async_copy(src.at[:, columns(j)], ubuf.at[slot, part], usem.at[slot, part])
+            for part, src in enumerate((sg, su))
+        ]
+
     def h_copy(e):
         return pltpu.make_async_copy(h_hbm.at[e], h.at[e], lsem.at[e])
 
@@ -338,22 +311,16 @@
         return pltpu.make_async_copy(yst.at[slot], y_hbm.at[:, columns(t)], ysem.at[slot])
 
     load_ct = pltpu.make_async_copy(ct_hbm, ct, lsem.at[own])
-    load_hs = pltpu.make_async_copy(hs_hbm, hs, lsem.at[own + 1])
+    load_x = pltpu.make_async_copy(x_hbm, x, lsem.at[own + 1])
 
     for e in range(own):
         h_copy(e).start()
         if e < ring - BATCH:
             w_copy(jnp.int32(e)).start()
     load_ct.start()
-    load_hs.start()
-    s_copy(jnp.int32(0)).start()
     greet((xn, yn, pn))
 
     def compute(t):
-        @pl.when(t + 1 < tiles)
-        def _():
-            s_copy(t + 1).start()
-
         def experts(i, _):
             @pl.when(jnp.logical_and(i == 1, t >= 1))
             def _():
@@ -389,19 +356,45 @@
 
         @pl.when(t == 0)
         def _():
+            load_x.start()
+            for j in range(2):
+                for copy in u_copies(jnp.int32(j)):
+                    copy.start()
+                s_copy(jnp.int32(j)).start()
             load_ct.wait()
-            load_hs.wait()
 
         def terms(q):
             return lax.dot_general(ct[q], out[q], (((0,), (0,)), ((), ())), preferred_element_type=F32)
 
+        @pl.when(t >= 3)
+        def _():
+            to_partner(t - 3).wait_send()
+
         for q in range(4, 8):
-            dsend[t, q - 4] = terms(q).astype(BF16)
+            dsend[lax.rem(t, 3), q - 4] = terms(q).astype(BF16)
         to_partner(t).start()
+        for q in range(4):
+            keep[t, q] = terms(q)
+
+    def shared_up(j):
+        for copy in u_copies(j):
+            copy.wait()
+        slot = lax.rem(j, 2)
+        a, b = (dot(x[...], ubuf[slot, part]) for part in range(2))
+        hs[:, columns(j)] = (jax.nn.silu(a) * b).astype(BF16)
+
+        @pl.when(j + 2 < slices)
+        def _():
+            for copy in u_copies(j + 2):
+                copy.start()
+
+    def shared_down(t):
         s_copy(t).wait()
-        keep[t, 0] = terms(0) + dot(hs[...], sbuf[lax.rem(t, 2)])
-        for q in range(1, 4):
-            keep[t, q] = terms(q)
+        keep[t, 0] = keep[t, 0] + dot(hs[...], sbuf[lax.rem(t, 2)])
+
+        @pl.when(t + 2 < tiles)
+        def _():
+            s_copy(t + 2).start()
 
     def stage_one(t):
         to_partner(t).wait_recv()
@@ -447,17 +440,37 @@
         def _():
             compute(t)
 
+        @pl.when(t == 1)
+        def _():
+            load_x.wait()
+
+        @pl.when(jnp.logical_and(t >= 1, t < tiles - 1))
+        def _():
+            for i in range(2):
+
+                @pl.when(2 * t - 2 + i < slices)
+                def _():
+                    shared_up(2 * t - 2 + i)
+
         @pl.when(t == tiles)
         def _():
             stage_one(t - 1)
 
+        late = 2 * (t - (tiles - 1))
+
+        @pl.when(late >= 0)
+        def _():
+            shared_down(late)
+            shared_down(late + 1)
+
         @pl.when(jnp.logical_and(t >= tiles, t <= tiles + 1))
         def _():
             stage_two(t - 2)
 
-        @pl.when(t >= 3)
-        def _():
-            stage_three(t - 3)
+        @pl.when(late >= 0)
+        def _():
+            stage_three(late)
+            stage_three(late + 1)
 
         return 0
 
@@ -466,9 +479,12 @@
         y_copy(jnp.int32(t)).wait()
 
     def drain(t, _):
-        for copy in (to_partner(t), *phase_one(t), *phase_two(t)):
+        for copy in (*phase_one(t), *phase_two(t)):
             copy.wait_send()
         return 0
+
+    for t in range(tiles - 3, tiles):
+        to_partner(jnp.int32(t)).wait_send()
 
     lax.fori_loop(0, tiles, drain, 0)
 
@@ -490,15 +506,14 @@
         pieces, ring = 8, 8
         width = d // pieces
         rows = own * PAD
-        h, hs, ct = pl.pallas_call(
+        h, ct = pl.pallas_call(
             functools.partial(first_kernel, (pieces, width, tokens, ff, own, ring)),
             out_shape=(
                 jax.ShapeDtypeStruct((own, rows, ff), BF16),
-                jax.ShapeDtypeStruct((tokens, 2 * ff), BF16),
                 jax.ShapeDtypeStruct((8, rows, tokens), BF16),
             ),
-            in_specs=[hbm] * 6,
-            out_specs=(hbm,) * 3,
+            in_specs=[hbm] * 4,
+            out_specs=(hbm,) * 2,
             scratch_shapes=[
                 pltpu.VMEM((pieces, 8, tokens, width), BF16),
                 pltpu.VMEM((8, 16, tokens), F32),
@@ -519,24 +534,26 @@
                 collective_id=0, has_side_effects=True, vmem_limit_bytes=VMEM_BYTES
             ),
             name="dispatch_up",
-        )(x, meta, w_gate, w_up, s_gate, s_up)
+        )(x, meta, w_gate, w_up)
 
         tiles, ring = 8, 12
         width = d // tiles
         y = pl.pallas_call(
             functools.partial(second_kernel, (tiles, width, tokens, own, ring)),
             out_shape=jax.ShapeDtypeStruct((tokens, d), BF16),
-            in_specs=[hbm] * 5,
+            in_specs=[hbm] * 7,
             out_specs=hbm,
             scratch_shapes=[
                 pltpu.VMEM((own, rows, ff), BF16),
+                pltpu.VMEM((8, rows, tokens), BF16),
+                pltpu.VMEM((tokens, d), BF16),
                 pltpu.VMEM((tokens, 2 * ff), BF16),
-                pltpu.VMEM((8, rows, tokens), BF16),
                 pltpu.VMEM((ring, ff, width), BF16),
+                pltpu.VMEM((2, 2, d, width), BF16),
                 pltpu.VMEM((2, 2 * ff, width), BF16),
                 pltpu.VMEM((8, rows, width), BF16),
                 pltpu.VMEM((tiles, 4, tokens, width), F32),
-                pltpu.VMEM((tiles, 4, tokens, width), BF16),
+                pltpu.VMEM((3, 4, tokens, width), BF16),
                 pltpu.VMEM((tiles, 4, tokens, width), BF16),
                 pltpu.VMEM((tiles, 4, tokens // 2, width), BF16),
                 pltpu.VMEM((tiles, 4, tokens // 2, width), BF16),
@@ -545,6 +562,7 @@
                 pltpu.VMEM((2, tokens, width), BF16),
                 dma((own + 2,)),
                 dma((ring,)),
+                dma((2, 2)),
                 dma((2,)),
                 dma((2,)),
                 dma((tiles, 5)),
@@ -554,7 +572,7 @@
                 collective_id=1, has_side_effects=True, vmem_limit_bytes=VMEM_BYTES
             ),
             name="down_combine",
-        )(h, hs, ct, w_down, s_down)
+        )(h, ct, x, w_down, s_gate, s_up, s_down)
         return y[None, None]
 
     tok, exp, rep = P("dp", "ep"), P("ep"), P()

time: 153 us -> 151 us (0.987)
  Pallas kernels: 148 us -> 146 us
    pallas_call x1, Pallas kernels: 80.6 us -> 78.5 us  [body(): pl.pallas_call(functools.partial(first_kernel, (pieces, width, tokens, ff...]
where the time goes in v3:
time: 151 us; the launch traced here: 150 us
  Pallas kernels  146 us (97%)
  local copies, waits for them, and re-layouts  3.43 us (2%)
    pallas_call x1, Pallas kernels, body(): pl.pallas_call(functools.partial(first_kernel, (pieces, width, tokens, ff...  78.5 us
    pallas_call x1, Pallas kernels, body(): pl.pallas_call(functools.partial(second_kernel, (tiles, width, tokens, ow...  67 us
    unnamed x2, local copies, waits for them, and re-layouts  3.43 us

profile of v3, /device:TPU:0, one launch (start us, length us, event | category | flops | bytes accessed | tf_op | source)
XLA Modules:
  0.0 150.4 jit_solution(13962095320286504957)
XLA Ops:
  0.0 0.7 fusion.2
  0.7 0.7 copy.29
  1.4 0.6 select_maximum_fusion.meta_hbm
  2.0 78.5 %dispatch_up.1 = (bf16[8,384,1408]{2,1,0:T(8,128)(2,1)}, bf16[8,384,384]{2,1,0:T(8,128)(2,1)}) custom-call(bf16[384,2048]{1,0:T(8,128)(2,1)} %bitcast.12, f32[16,384]{1,0:T(8,128)} %select_maximum_fusion.meta_hbm, bf16[8,2048,1408]{2,1,0:T(8,128)(2,1)} %wg.1, bf16[8,2048,1408]{2,1,0:T(8,128)(2,1)} %wu.1), custom_call_target="tpu_custom_call" | custom-call | tf_op jit(solution)/shard_map/dispatch_up/pallas_call | solution.py:509
  80.6 67.0 %down_combine.1 = bf16[384,2048]{1,0:T(8,128)(2,1)} custom-call(bf16[8,384,1408]{2,1,0:T(8,128)(2,1)} %get-tuple-element.7.h_hbm, bf16[8,384,384]{2,1,0:T(8,128)(2,1)} %get-tuple-element.8.ct_hbm, bf16[384,2048]{1,0:T(8,128)(2,1)} %bitcast.13, bf16[8,1408,2048]{2,1,0:T(8,128)(2,1)} %wd.1, bf16[2048,2816]{1,0:T(8,128)(2,1)} %sg.1, bf16[2048,2816]{1,0:T(8,128)(2,1)} %su.1, ...), custom_call_target="tpu_custom_call" | custom-call | tf_op jit(solution)/shard_map/down_combine/pallas_call | solution.py:541
  147.6 2.7 %copy.31 = bf16[1,1,384,2048]{3,2,1,0:T(8,128)(2,1)} copy(bf16[1,1,384,2048]{3,2,1,0:T(8,128)(2,1)} %bitcast.11) | data formatting | bytes 3145728

commit v4 on v3

--- a/solution.py
+++ b/solution.py
@@ -12,7 +12,8 @@
 VMEM_BYTES = 67043328
 GROUP, BATCH = 4, 4
 PAD = 48
-OWN, NEAR, FAR, RELAY, LAST, PARTNER = (0, 1, 2), (0, 1), (3, 4), (3, 4, 5, 6), (7,), (2, 5, 6, 7)
+OWN_A, OWN_B, RELAY, FORWARD, LAST, PARTNER = (0, 2, 4), (1, 3), (5, 6), (7, 8), (9,), (4, 7, 8, 9)
+NEAR_A, NEAR_B, FAR = (0, 2), (1, 3), (5, 6)
 
 
 def neighbours():
@@ -50,7 +51,8 @@
         mid = rows // 2
         low, high = pl.ds(0, mid), pl.ds(mid, mid)
         plan = (
-            (ref(0), ref(1), xn), (ref(0), ref(2), yn), (ref(0), ref(4), pn),
+            (ref(0).at[low], ref(1).at[low], xn), (ref(0).at[high], ref(1).at[high], xn),
+            (ref(0).at[high], ref(2).at[high], yn), (ref(0).at[low], ref(2).at[low], yn), (ref(0), ref(4), pn),
             (ref(1).at[low], ref(3).at[low], yn), (ref(2).at[high], ref(3).at[high], xn),
             (ref(1), ref(5), pn), (ref(2), ref(6), pn), (ref(3), ref(7), pn),
         )
@@ -110,7 +112,8 @@
     load_meta.wait()
     start(of_meta())
     load_x(0).wait()
-    start(of_x(0, OWN))
+    start(of_x(0, OWN_A))
+    start(of_x(0, OWN_B))
     for g in range(ring - GROUP):
         fetch(jnp.int32(g))
     for c in range(1, pieces):
@@ -125,8 +128,22 @@
         return slots
 
     def relay(c):
-        await_recv(of_x(c, NEAR))
+        await_recv(of_x(c, NEAR_A))
         start(of_x(c, RELAY))
+
+        @pl.when(c + 1 < pieces)
+        def _():
+            start(of_x(c + 1, OWN_B))
+
+        @pl.when(c + 2 < pieces)
+        def _():
+            start(of_x(c + 2, OWN_A))
+
+    await_recv(of_x(0, NEAR_A))
+    start(of_x(0, RELAY))
+    start(of_x(1, OWN_A))
+    start(of_x(1, OWN_B))
+    start(of_x(2, OWN_A))
 
     await_recv(of_meta())
     base = (me * (own * PAD)).astype(F32)
@@ -172,10 +189,8 @@
         def _():
             relay(c + 1)
 
-        @pl.when(c + 3 < pieces)
-        def _():
-            start(of_x(c + 3, OWN))
-
+        await_recv(of_x(c, NEAR_B))
+        start(of_x(c, FORWARD))
         await_recv(of_x(c, FAR))
         start(of_x(c, LAST))
 
@@ -183,11 +198,7 @@
         def experts(i, _):
             @pl.when(i == 1)
             def _():
-                if new:
-                    relay(1)
-                    start(of_x(3, OWN))
-                else:
-                    pass_on(c + 1)
+                pass_on(c + 1)
 
             slots = take(c * own // GROUP + i)
             for j, slot in enumerate(slots):
@@ -199,16 +210,10 @@
             return 0
 
         lax.fori_loop(0, own // GROUP, experts, 0)
-        if new:
-            pass_on(c + 1)
         gather(c + 1)
         return 0
 
-    relay(0)
-    for c in (1, 2):
-        start(of_x(c, OWN))
-    await_recv(of_x(0, FAR))
-    start(of_x(0, LAST))
+    pass_on(jnp.int32(0))
     gather(0)
     piece(jnp.int32(0), 0, True)
     lax.fori_loop(1, pieces - 1, functools.partial(piece, new=False), 0)
@@ -243,7 +248,7 @@
         out_h(jnp.int32(e)).wait()
 
     def drain(c, _):
-        for copy in of_x(c, range(8)):
+        for copy in of_x(c, range(10)):
             copy.wait_send()
         return 0
 
@@ -527,8 +532,8 @@
                 dma((ring, 2)),
                 dma((2,)),
                 dma((2,)),
-                dma((pieces + 1, 8)),
-                dma((pieces + 1, 8)),
+                dma((pieces + 1, 10)),
+                dma((pieces + 1, 10)),
             ],
             compiler_params=pltpu.CompilerParams(
                 collective_id=0, has_side_effects=True, vmem_limit_bytes=VMEM_BYTES

time: 151 us -> 147 us (0.974)
  Pallas kernels: 146 us -> 142 us
    pallas_call x1, Pallas kernels: 78.5 us -> 75.1 us  [body(): pl.pallas_call(functools.partial(first_kernel, (pieces, width, tokens, ff...]
where the time goes in v4:
time: 147 us
  Pallas kernels  142 us (97%)
  local copies, waits for them, and re-layouts  3.43 us (2%)
    pallas_call x1, Pallas kernels, body(): pl.pallas_call(functools.partial(first_kernel, (pieces, width, tokens, ff...  75.1 us
    pallas_call x1, Pallas kernels, body(): pl.pallas_call(functools.partial(second_kernel, (tiles, width, tokens, ow...  66.6 us
    unnamed x2, local copies, waits for them, and re-layouts  3.43 us

profile of v4, /device:TPU:0, one launch (start us, length us, event | category | flops | bytes accessed | tf_op | source)
XLA Modules:
  0.0 146.5 jit_solution(2638580352168485672)
XLA Ops:
  0.0 0.7 fusion.2
  0.7 0.7 copy.29
  1.4 0.6 select_maximum_fusion.meta_hbm
  2.0 75.1 %dispatch_up.1 = (bf16[8,384,1408]{2,1,0:T(8,128)(2,1)}, bf16[8,384,384]{2,1,0:T(8,128)(2,1)}) custom-call(bf16[384,2048]{1,0:T(8,128)(2,1)} %bitcast.12, f32[16,384]{1,0:T(8,128)} %select_maximum_fusion.meta_hbm, bf16[8,2048,1408]{2,1,0:T(8,128)(2,1)} %wg.1, bf16[8,2048,1408]{2,1,0:T(8,128)(2,1)} %wu.1), custom_call_target="tpu_custom_call" | custom-call | tf_op jit(solution)/shard_map/dispatch_up/pallas_call | solution.py:514
  77.1 66.6 %down_combine.1 = bf16[384,2048]{1,0:T(8,128)(2,1)} custom-call(bf16[8,384,1408]{2,1,0:T(8,128)(2,1)} %get-tuple-element.7.h_hbm, bf16[8,384,384]{2,1,0:T(8,128)(2,1)} %get-tuple-element.8.ct_hbm, bf16[384,2048]{1,0:T(8,128)(2,1)} %bitcast.13, bf16[8,1408,2048]{2,1,0:T(8,128)(2,1)} %wd.1, bf16[2048,2816]{1,0:T(8,128)(2,1)} %sg.1, bf16[2048,2816]{1,0:T(8,128)(2,1)} %su.1, ...), custom_call_target="tpu_custom_call" | custom-call | tf_op jit(solution)/shard_map/down_combine/pallas_call | solution.py:546
  143.8 2.7 %copy.31 = bf16[1,1,384,2048]{3,2,1,0:T(8,128)(2,1)} copy(bf16[1,1,384,2048]{3,2,1,0:T(8,128)(2,1)} %bitcast.11) | data formatting | bytes 3145728

commit v5 on v4

--- a/solution.py
+++ b/solution.py
@@ -22,10 +22,11 @@
     return me, me + 4 - 8 * x, me + 2 - 4 * y, me + 1 - 2 * core
 
 
-def greet(devices):
+def greet(devices, meanwhile=lambda: None):
     barrier = pltpu.get_barrier_semaphore()
     for device in devices:
         pl.semaphore_signal(barrier, inc=1, device_id={"ep": device}, device_id_type=MESH)
+    meanwhile()
     pl.semaphore_wait(barrier, len(devices))
 
 
@@ -38,10 +39,10 @@
 
 
 def first_kernel(
-    dims, x_hbm, meta_hbm, wg, wu, h_out, ct_out,
-    xg, meta, acc, wbuf, z, pm, stage, ctst, xsem, wsem, osem, csem, send, recv,
+    dims, x_hbm, expert_hbm, slot_hbm, gate_hbm, wg, wu, h_out, ct_out,
+    xg, ids, gates, meta, acc, wbuf, z, pm, stage, ctst, xsem, wsem, osem, csem, send, recv,
 ):
-    pieces, width, tokens, ff, own, ring = dims
+    pieces, width, tokens, ff, own, ring, slots_each, top = dims
     me, xn, yn, pn = neighbours()
     dn = xn + yn - me
     others = [xn, yn, dn] + [device + pn - me for device in (me, xn, yn, dn)]
@@ -87,7 +88,10 @@
     def load_x(c):
         return pltpu.make_async_copy(x_hbm.at[:, pl.ds(c * width, width)], xg.at[c, 0], xsem.at[c])
 
-    load_meta = pltpu.make_async_copy(meta_hbm, meta.at[0], xsem.at[pieces])
+    load_meta = [
+        pltpu.make_async_copy(src, dst, xsem.at[pieces + i])
+        for i, (src, dst) in enumerate(((expert_hbm, ids.at[0]), (slot_hbm, ids.at[1]), (gate_hbm, gates)))
+    ]
 
     def w_copy(src, slot, part):
         return pltpu.make_async_copy(src, wbuf.at[slot, :, pl.ds(part * ff, ff)], wsem.at[slot, part])
@@ -105,11 +109,20 @@
         for part in range(2):
             w_copy(wg.at[0, pl.ds(0, width)], slot, part).wait()
 
-    load_meta.start()
+    start(load_meta)
     for c in range(pieces):
         load_x(c).start()
-    greet(others)
-    load_meta.wait()
+    def fill_meta():
+        meta[0] = jnp.zeros((16, tokens), F32)
+        for copy in load_meta:
+            copy.wait()
+        for j in range(top):
+            slot = ids[1, j]
+            place = jnp.where(slot < slots_each, ids[0, j] * PAD + slot, -1)
+            meta[0, j : j + 1] = place.astype(F32)
+            meta[0, 8 + j : 9 + j] = gates[j]
+
+    greet(others, fill_meta)
     start(of_meta())
     load_x(0).wait()
     start(of_x(0, OWN_A))
@@ -161,7 +174,7 @@
         for e in range(own):
             p = jnp.zeros((PAD, tokens), F32)
             c = jnp.zeros((PAD, tokens), F32)
-            for j in range(6):
+            for j in range(top):
                 hit = (place[j : j + 1] - float(e * PAD)) == row
                 p = jnp.where(hit, 1.0, p)
                 c = jnp.where(hit, gate[j : j + 1], c)
@@ -501,10 +514,8 @@
         tokens, top = expert.shape[2:]
         own, d, ff = w_gate.shape
         slots = 5 * tokens * top // (4 * own * members)
-        x, expert, slot, gate = x[0, 0], expert[0, 0], slot[0, 0], gate[0, 0]
-        place = jnp.where(slot < slots, expert * PAD + slot, -1).astype(F32)
-        fill = ((0, 8 - top), (0, 0))
-        meta = jnp.concatenate([jnp.pad(place.T, fill, constant_values=-1.0), jnp.pad(gate.T, fill)])
+        x = x[0, 0]
+        expert, slot, gate = (v.transpose(3, 0, 1, 2).reshape(top, 1, tokens) for v in (expert, slot, gate))
 
         hbm = pl.BlockSpec(memory_space=pl.ANY)
         dma = pltpu.SemaphoreType.DMA
@@ -512,15 +523,17 @@
         width = d // pieces
         rows = own * PAD
         h, ct = pl.pallas_call(
-            functools.partial(first_kernel, (pieces, width, tokens, ff, own, ring)),
+            functools.partial(first_kernel, (pieces, width, tokens, ff, own, ring, slots, top)),
             out_shape=(
                 jax.ShapeDtypeStruct((own, rows, ff), BF16),
                 jax.ShapeDtypeStruct((8, rows, tokens), BF16),
             ),
-            in_specs=[hbm] * 4,
+            in_specs=[hbm] * 6,
             out_specs=(hbm,) * 2,
             scratch_shapes=[
                 pltpu.VMEM((pieces, 8, tokens, width), BF16),
+                pltpu.VMEM((2, top, 1, tokens), jnp.int32),
+                pltpu.VMEM((top, 1, tokens), F32),
                 pltpu.VMEM((8, 16, tokens), F32),
                 pltpu.VMEM((own, rows, 2 * ff), F32),
                 pltpu.VMEM((ring, width, 2 * ff), BF16),
@@ -528,7 +541,7 @@
                 pltpu.VMEM((8, rows, tokens), BF16),
                 pltpu.VMEM((2, rows, ff), BF16),
                 pltpu.VMEM((2, rows, tokens), BF16),
-                dma((pieces + 1,)),
+                dma((pieces + 3,)),
                 dma((ring, 2)),
                 dma((2,)),
                 dma((2,)),
@@ -539,7 +552,7 @@
                 collective_id=0, has_side_effects=True, vmem_limit_bytes=VMEM_BYTES
             ),
             name="dispatch_up",
-        )(x, meta, w_gate, w_up)
+        )(x, expert, slot, gate, w_gate, w_up)
 
         tiles, ring = 8, 12
         width = d // tiles

time: 147 us -> 145 us (0.986)
    unnamed x2 -> x1, local copies, waits for them, and re-layouts: 3.43 us -> 2.73 us
where the time goes in v5:
time: 145 us; the launch traced here: 144 us
  Pallas kernels  142 us (98%)
  local copies, waits for them, and re-layouts  2.73 us (2%)
    pallas_call x1, Pallas kernels, body(): pl.pallas_call(functools.partial(first_kernel, (pieces, width, tokens, ff...  75.1 us
    pallas_call x1, Pallas kernels, body(): pl.pallas_call(functools.partial(second_kernel, (tiles, width, tokens, ow...  66.6 us

profile of v5, /device:TPU:0, one launch (start us, length us, event | category | flops | bytes accessed | tf_op | source)
XLA Modules:
  0.0 144.5 jit_solution(2828481659934473437)
XLA Ops:
  0.0 75.1 %dispatch_up.1 = (bf16[8,384,1408]{2,1,0:T(8,128)(2,1)}, bf16[8,384,384]{2,1,0:T(8,128)(2,1)}) custom-call(bf16[384,2048]{1,0:T(8,128)(2,1)} %bitcast.18, s32[6,1,384]{2,1,0:T(1,128)} %bitcast.20, s32[6,1,384]{2,1,0:T(1,128)} %bitcast.21, f32[6,1,384]{2,1,0:T(1,128)} %bitcast.22, bf16[8,2048,1408]{2,1,0:T(8,128)(2,1)} %wg.1, bf16[8,2048,1408]{2,1,0:T(8,128)(2,1)} %wu.1), custom_call_target="tpu_custom_call" | custom-call | tf_op jit(solution)/shard_map/dispatch_up/pallas_call | solution.py:525
  75.1 66.6 %down_combine.1 = bf16[384,2048]{1,0:T(8,128)(2,1)} custom-call(bf16[8,384,1408]{2,1,0:T(8,128)(2,1)} %get-tuple-element.7.h_hbm, bf16[8,384,384]{2,1,0:T(8,128)(2,1)} %get-tuple-element.8.ct_hbm, bf16[384,2048]{1,0:T(8,128)(2,1)} %bitcast.19, bf16[8,1408,2048]{2,1,0:T(8,128)(2,1)} %wd.1, bf16[2048,2816]{1,0:T(8,128)(2,1)} %sg.1, bf16[2048,2816]{1,0:T(8,128)(2,1)} %su.1, ...), custom_call_target="tpu_custom_call" | custom-call | tf_op jit(solution)/shard_map/down_combine/pallas_call | solution.py:559
  141.8 2.7 %copy.15 = bf16[1,1,384,2048]{3,2,1,0:T(8,128)(2,1)} copy(bf16[1,1,384,2048]{3,2,1,0:T(8,128)(2,1)} %bitcast.17) | data formatting | bytes 3145728

commit v6 on v5

--- a/solution.py
+++ b/solution.py
@@ -291,11 +291,10 @@
         return remote(t, 0, dsend.at[lax.rem(t, 3)], drecv.at[t], pn)
 
     def phase_one(t):
-        a, b = pl.ds(0, 2), pl.ds(2, 2)
-        return (
-            remote(t, 1, s1.at[t, a], r1.at[t, a], xn),
-            remote(t, 2, s1.at[t, b], r1.at[t, b], yn),
-        )
+        return [
+            remote(t, kind, s1.at[t, i], r1.at[t, i], device)
+            for kind, i, device in ((1, 1, xn), (2, 3, yn), (5, 0, xn), (6, 2, yn))
+        ]
 
     def phase_two(t):
         return (
@@ -431,12 +430,15 @@
         keep[t, 2, low] = both(2, low)
 
     def stage_two(t):
-        for copy in phase_one(t):
+        arrivals = phase_one(t)
+        for copy in arrivals[:2]:
             copy.wait_recv()
         s2[t, 0] = (keep[t, 2, low] + r1[t, 1].astype(F32)).astype(BF16)
         s2[t, 1] = (keep[t, 1, high] + r1[t, 3].astype(F32)).astype(BF16)
         for copy in phase_two(t):
             copy.start()
+        for copy in arrivals[2:]:
+            copy.wait_recv()
         keep[t, 0, low] = keep[t, 0, low] + r1[t, 0].astype(F32)
         keep[t, 0, high] = keep[t, 0, high] + r1[t, 2].astype(F32)
 
@@ -583,8 +585,8 @@
                 dma((2, 2)),
                 dma((2,)),
                 dma((2,)),
-                dma((tiles, 5)),
-                dma((tiles, 5)),
+                dma((tiles, 7)),
+                dma((tiles, 7)),
             ],
             compiler_params=pltpu.CompilerParams(
                 collective_id=1, has_side_effects=True, vmem_limit_bytes=VMEM_BYTES

time: 145 us -> 145 us (level)
  no operation moved by 1% of the time
where the time goes in v6:
time: 145 us
  Pallas kernels  142 us (98%)
  local copies, waits for them, and re-layouts  2.73 us (2%)
    pallas_call x1, Pallas kernels, body(): pl.pallas_call(functools.partial(first_kernel, (pieces, width, tokens, ff...  75.1 us
    pallas_call x1, Pallas kernels, body(): pl.pallas_call(functools.partial(second_kernel, (tiles, width, tokens, ow...  66.8 us

profile of v6, /device:TPU:0, one launch (start us, length us, event | category | flops | bytes accessed | tf_op | source)
XLA Modules:
  0.0 144.7 jit_solution(13086543852062750386)
XLA Ops:
  0.0 75.1 %dispatch_up.1 = (bf16[8,384,1408]{2,1,0:T(8,128)(2,1)}, bf16[8,384,384]{2,1,0:T(8,128)(2,1)}) custom-call(bf16[384,2048]{1,0:T(8,128)(2,1)} %bitcast.18, s32[6,1,384]{2,1,0:T(1,128)} %bitcast.20, s32[6,1,384]{2,1,0:T(1,128)} %bitcast.21, f32[6,1,384]{2,1,0:T(1,128)} %bitcast.22, bf16[8,2048,1408]{2,1,0:T(8,128)(2,1)} %wg.1, bf16[8,2048,1408]{2,1,0:T(8,128)(2,1)} %wu.1), custom_call_target="tpu_custom_call" | custom-call | tf_op jit(solution)/shard_map/dispatch_up/pallas_call | solution.py:527
  75.1 66.8 %down_combine.1 = bf16[384,2048]{1,0:T(8,128)(2,1)} custom-call(bf16[8,384,1408]{2,1,0:T(8,128)(2,1)} %get-tuple-element.7.h_hbm, bf16[8,384,384]{2,1,0:T(8,128)(2,1)} %get-tuple-element.8.ct_hbm, bf16[384,2048]{1,0:T(8,128)(2,1)} %bitcast.19, bf16[8,1408,2048]{2,1,0:T(8,128)(2,1)} %wd.1, bf16[2048,2816]{1,0:T(8,128)(2,1)} %sg.1, bf16[2048,2816]{1,0:T(8,128)(2,1)} %su.1, ...), custom_call_target="tpu_custom_call" | custom-call | tf_op jit(solution)/shard_map/down_combine/pallas_call | solution.py:561
  141.9 2.7 %copy.15 = bf16[1,1,384,2048]{3,2,1,0:T(8,128)(2,1)} copy(bf16[1,1,384,2048]{3,2,1,0:T(8,128)(2,1)} %bitcast.17) | data formatting | bytes 3145728
